TPU v7x, 32 devices: a whole 2x2x4 slice. The times are simulated.
32 devices in a mesh: dp: 4 (over z), fsdp: 8 (over y, x, core).
Axes of the slice: x: 2, y: 2, z: 4, core: 2. Of those that a mesh axis runs over, the one named last changes fastest.
Arguments:
- hidden: bfloat16 [8192, 4096], P(('dp', 'fsdp')), may hold values from -6 to 6
- queries: bfloat16 [8192, 2048], P(('dp', 'fsdp')), may hold values from -6 to 6
- keys: bfloat16 [8192, 512], P(('dp', 'fsdp')), may hold values from -6 to 6
- target: bfloat16 [8192, 2048], P(('dp', 'fsdp')), may hold values from -6 to 6
- lengths: int32 [32], P(('dp', 'fsdp')), may hold values from 64 to 256
- value_weight_frozen: bfloat16 [4096, 512], P('fsdp'), may hold values from -0.09375 to 0.09375
- adapter_down_map: float32 [4096, 64], P('fsdp'), may hold values from -0.09375 to 0.09375
- adapter_up_map: float32 [64, 512], replicated, may hold values from -0.75 to 0.75
- average_down_map: float32 [4096, 64], P('fsdp'), may hold values from -0.09375 to 0.09375
- average_up_map: float32 [64, 512], replicated, may hold values from -0.75 to 0.75
Outputs:
- down_map_gradient: float32 [4096, 64], P('fsdp')
- up_map_gradient: float32 [64, 512], replicated
- average_down_next: float32 [4096, 64], P('fsdp')
- average_up_next: float32 [64, 512], replicated
- loss: float32 [], replicated
Inputs may be any that keep to these rules, and one draw needn't show every extreme that they name: `lengths`: slots at or past a sequence's length are padding.
All inputs are finite; a program needn't handle non-finite values.
Results may differ from a plain program's by a relative error of at most 0.0049.
Values may be sent and summed in bfloat16 or wider, within the bound.
A program may use at most 64 MiB of HBM per device.

v0:
```python
import math
import jax
import jax.numpy as jnp
from jax import lax
from jax.sharding import PartitionSpec as P

HEADS = 16
KEY_VALUE_HEADS = 4
HEAD_DIM = 128
adapter_scale = 2.0
average_decay = 0.9
learning_rate = 1.0
masked_score = -1e30


def per_device(
    hidden,
    queries,
    keys,
    target,
    lengths,
    value_weight_frozen,
    adapter_down_map,
    adapter_up_map,
    average_down_map,
    average_up_map,
):
    tok_rows = hidden.shape[0]
    group_size = HEADS // KEY_VALUE_HEADS
    seq_length = lengths[0]
    down_factor_slice = adapter_down_map.astype(jnp.bfloat16)
    up_factor_slice = adapter_up_map.astype(jnp.bfloat16)
    columns = hidden
    frozen_value_output = jnp.dot(
        columns,
        lax.all_gather(value_weight_frozen, "fsdp", axis=0, tiled=True),
        preferred_element_type=jnp.float32,
    )
    adapter_hidden = jnp.dot(
        columns,
        lax.all_gather(down_factor_slice, "fsdp", axis=0, tiled=True),
        preferred_element_type=jnp.float32,
    )
    adapter_hidden = adapter_hidden.astype(jnp.bfloat16)
    value_outputs = (
        frozen_value_output
        + adapter_scale
        * jnp.dot(adapter_hidden, up_factor_slice, preferred_element_type=jnp.float32)
    ).astype(jnp.bfloat16)
    position = jnp.arange(tok_rows, dtype=jnp.int32)
    allowed = (position[None, :] <= position[:, None]) & (position[None, :] < seq_length)
    q_heads = queries.reshape(tok_rows, KEY_VALUE_HEADS, group_size, HEAD_DIM)
    k_heads = keys.reshape(tok_rows, KEY_VALUE_HEADS, HEAD_DIM)
    v_heads = value_outputs.reshape(tok_rows, KEY_VALUE_HEADS, HEAD_DIM)
    scores = jnp.einsum(
        "tkgd,skd->kgts", q_heads, k_heads, preferred_element_type=jnp.float32
    ) / math.sqrt(HEAD_DIM)
    scores = jnp.where(allowed, scores, masked_score)
    row_max = jnp.max(scores, axis=-1, keepdims=True)
    weights = jnp.exp(scores - row_max)
    attn_probs = (weights / jnp.sum(weights, axis=-1, keepdims=True)).astype(jnp.bfloat16)
    output = jnp.einsum(
        "kgts,skd->tkgd", attn_probs, v_heads, preferred_element_type=jnp.float32
    ).reshape(tok_rows, HEADS * HEAD_DIM)
    live_rows = (position < seq_length)[:, None]
    differ = jnp.where(live_rows, output - target.astype(jnp.float32), 0.0)
    loss_local = jnp.sum(differ * differ)
    cotangent = differ.astype(jnp.bfloat16).reshape(tok_rows, KEY_VALUE_HEADS, group_size, HEAD_DIM)
    value_grad = jnp.einsum(
        "kgts,tkgd->skd", attn_probs, cotangent, preferred_element_type=jnp.float32
    )
    value_grad = value_grad.reshape(tok_rows, KEY_VALUE_HEADS * HEAD_DIM).astype(jnp.bfloat16)
    latent_grad = lax.dot_general(
        value_grad, up_factor_slice, (((1,), (1,)), ((), ())), preferred_element_type=jnp.float32
    ).astype(jnp.bfloat16)
    up_term = lax.dot_general(
        adapter_hidden, value_grad, (((0,), (0,)), ((), ())), preferred_element_type=jnp.float32
    )
    count_local = seq_length.astype(jnp.float32)
    columns = hidden
    down_map_gradient = lax.psum(
        adapter_scale
        * lax.dot_general(
            columns, latent_grad, (((0,), (0,)), ((), ())), preferred_element_type=jnp.float32
        ),
        "dp",
    )
    down_map_gradient = lax.psum_scatter(down_map_gradient, "fsdp", scatter_dimension=0, tiled=True)
    up_map_gradient, loss_sum, token_grand_count = lax.psum(
        (adapter_scale * up_term, loss_local, count_local), ("dp", "fsdp")
    )
    up_map_gradient = up_map_gradient / token_grand_count
    down_map_gradient = down_map_gradient / token_grand_count
    loss = loss_sum / (2.0 * token_grand_count)
    average_down_next = average_decay * average_down_map + (1.0 - average_decay) * (
        adapter_down_map - learning_rate * down_map_gradient
    )
    average_up_next = average_decay * average_up_map + (1.0 - average_decay) * (
        adapter_up_map - learning_rate * up_map_gradient
    )
    return (down_map_gradient, up_map_gradient, average_down_next, average_up_next, loss)


def solution(mesh):
    placed = (
        P(("dp", "fsdp"), None),
        P(("dp", "fsdp"), None),
        P(("dp", "fsdp"), None),
        P(("dp", "fsdp"), None),
        P(("dp", "fsdp")),
        P("fsdp", None),
        P("fsdp", None),
        P(),
        P("fsdp", None),
        P(),
    )
    return jax.shard_map(
        per_device,
        mesh=mesh,
        in_specs=placed,
        out_specs=(P("fsdp", None), P(), P("fsdp", None), P(), P()),
        check_vma=False,
    )
```

profile of v0, /device:TPU:0, one launch (start us, length us, event | category | flops | bytes accessed | tf_op | source)
XLA Modules:
  0.0 281.5 jit_solution(8382225691264275477)
XLA Ops:
  7.2 0.0 copy-start
  7.2 0.0 copy-start.3
  7.2 0.0 all-gather.2.cloned.1.call-start
  7.2 0.7 all-gather.2.cloned.1.call-update
  7.9 0.0 reduce-scatter.2.cloned.1.call-start
  8.6 1.8 reshape.40
  10.4 1.0 reshape.39
  11.4 0.0 copy-done.3
  11.5 11.3 %all_gather.7 = bf16[4096,64]{0,1:T(8,128)(2,1)S(1)} all-gather(bf16[512,64]{0,1:T(8,128)(2,1)S(1)} %convert_element_type.36), channel_id=1, replica_groups=mesh['dp'=4,'fsdp'=8] {'fsdp'}, dimensions={0}, use_global_device_ids=true | all-gather | bytes 589824 | tf_op jit(solution)/shard_map/all_gather | solution.py:41
  22.8 0.1 fusion.13
  22.9 0.0 copy-done
  22.9 1.4 convolution_convert_fusion.1
  24.3 0.7 fusion.10
  25.0 1.2 fusion.19
  26.3 1.8 divide_convert_fusion
  28.0 0.0 copy-start.1
  28.0 0.0 copy-start.5
  28.0 21.2 %all-gather.2.cloned.1.call-done = bf16[4096,512]{1,0:T(8,128)(2,1)} async-done(((bf16[512,512]{1,0:T(8,128)(2,1)}), bf16[4096,512]{1,0:T(8,128)(2,1)}) %all-gather.2.cloned.1.call-update) | async-done | bytes 4194320 | tf_op jit(solution)/shard_map/all_gather | solution.py:36
  49.2 3.4 %fusion.20 = f32[256,512]{1,0:T(8,128)S(1)} fusion(bf16[256,4096]{1,0:T(8,128)(2,1)S(1)} %copy-done, bf16[4096,512]{1,0:T(8,128)(2,1)} %all-gather.2.cloned.1.call-done), kind=kOutput, calls=%fused_computation.36 | convolution fusion | flops 1073741824 | bytes 6815744 | tf_op jit(solution)/shard_map/dot_general | solution.py:34
  52.7 0.0 copy-done.1
  52.7 0.0 copy-done.5
  52.7 0.3 fusion.8
  52.9 0.1 copy.27
  53.1 3.3 %fusion.21 = f32[4,128,4,256]{3,1,2,0:T(8,128)} fusion(bf16[256,4,128,1]{0,2,3,1:T(8,128)(2,1)S(1)} %bitcast.51, bf16[4,4,256,256]{2,3,1,0:T(8,128)(2,1)} %divide_convert_fusion), kind=kOutput, calls=%fused_computation.37 | convolution fusion | flops 268435456 | bytes 4456448 | tf_op jit(solution)/shard_map/kgts,skd->tkgd/dot_general | solution.py:62
  56.4 0.0 copy-start.2
  56.4 3.0 %copy.19 = f32[256,2048]{1,0:T(8,128)} copy(f32[256,2048]{0,1:T(8,128)} %bitcast.47) | data formatting | bytes 4194304 | tf_op jit(solution)/shard_map/reshape | solution.py:64
  59.5 0.0 copy-done.2
  59.5 3.6 %multiply_reduce_fusion = (f32[]{:T(128)}, bf16[256,2048]{1,0:T(8,128)(2,1)}) fusion(f32[256,2048]{1,0:T(8,128)} %copy.19, bf16[256,2048]{1,0:T(8,128)(2,1)S(1)} %copy-done.2, pred[256]{0:T(512)(128)(4,1)S(1)} %iota_compare_fusion.1), kind=kLoop, calls=%fused_computation.7 | loop fusion | flops 3145727 | bytes 4194564 | tf_op jit(solution)/shard_map/reduce_sum | solution.py:67
  63.1 1.5 copy.30
  64.6 2.4 fusion.9
  67.0 0.0 copy-start.6
  67.0 0.0 copy-start.7
  67.0 0.0 copy-start.4
  67.0 0.0 copy-start.8
  67.0 1.8 fusion.1
  68.9 0.0 reduce-scatter.2.cloned.1.call-update
  68.9 0.0 all-reduce.4.cloned.1.call-start
  68.9 0.0 copy-done.6
  69.0 0.9 convolution_multiply_fusion.2
  69.8 0.0 all-reduce.4.cloned.1.call-update
  69.8 0.0 all-reduce.6.cloned.1.call-start
  69.9 39.5 %all-reduce = (f32[]{:T(128)}, f32[]{:T(128)}) all-reduce(f32[]{:T(128)S(6)} %convert_element_type.47, f32[]{:T(128)} %get-tuple-element.11), channel_id=1, replica_groups=mesh['dp'=4,'fsdp'=8] {'dp','fsdp'}, use_global_device_ids=true, to_apply=%region_4.5 | all-reduce | flops 2 | bytes 16 | tf_op jit(solution)/shard_map/psum | solution.py:89
  110.7 0.0 reduce-scatter.2.cloned.1.call-done
  110.7 0.0 all-reduce.6.cloned.1.call-update
  110.7 125.1 %all-reduce.4.cloned.1.call-done = f32[64,512]{1,0:T(8,128)} async-done(((f32[64,512]{1,0:T(8,128)}), f32[64,512]{1,0:T(8,128)}) %all-reduce.4.cloned.1.call-update) | async-done | bytes 131088 | tf_op jit(solution)/shard_map/psum | solution.py:89
  235.8 0.0 copy-done.7
  235.8 2.2 multiply_add_fusion
  238.0 33.7 %all-reduce.6.cloned.1.call-done = f32[512,64]{0,1:T(8,128)} async-done(((f32[512,64]{0,1:T(8,128)}), f32[512,64]{0,1:T(8,128)}) %all-reduce.6.cloned.1.call-update) | async-done | bytes 131088 | tf_op jit(solution)/shard_map/psum | solution.py:81
  271.7 0.0 copy-done.4
  271.7 0.0 copy-done.8
  271.7 2.2 multiply_add_fusion.1
  (2 shorter events, 0.0 us)
Async XLA Ops:
  7.2 15.8 %copy-start = (bf16[256,4096]{1,0:T(8,128)(2,1)S(1)}, bf16[256,4096]{1,0:T(8,128)(2,1)}, u32[]{:S(2)}) copy-start(bf16[256,4096]{1,0:T(8,128)(2,1)} %param.10) | copy-start | bytes 6291460
  7.2 4.3 %copy-start.3 = (f32[512,64]{0,1:T(8,128)S(1)}, f32[512,64]{0,1:T(8,128)}, u32[]{:S(2)}) copy-start(f32[512,64]{0,1:T(8,128)} %param.16) | copy-start | bytes 393220
  7.2 42.0 %all-gather.2.cloned.1.call-start = ((), (), s32[]{:S(2)}) async-start(), calls=%async_computation.1 | async-start | bytes 4718592 | tf_op jit(solution)/shard_map/all_gather | solution.py:36
  7.9 102.8 %reduce-scatter.2.cloned.1.call-start = ((), (), s32[]{:S(2)}) async-start(), calls=%async_computation.3 | async-start | bytes 1179648 | tf_op jit(solution)/shard_map/reduce_scatter | solution.py:88
  28.0 24.6 %copy-start.1 = (f32[64,512]{1,0:T(8,128)S(1)}, f32[64,512]{1,0:T(8,128)}, u32[]{:S(2)}) copy-start(f32[64,512]{1,0:T(8,128)} %param.17) | copy-start | bytes 393220
  28.0 24.6 %copy-start.5 = (bf16[256,64]{0,1:T(8,128)(2,1)S(1)}, bf16[256,64]{0,1:T(8,128)(2,1)}, u32[]{:S(2)}) copy-start(bf16[256,64]{0,1:T(8,128)(2,1)} %convolution_convert_fusion.1) | copy-start | bytes 98308
  56.4 3.0 %copy-start.2 = (bf16[256,2048]{1,0:T(8,128)(2,1)S(1)}, bf16[256,2048]{1,0:T(8,128)(2,1)}, u32[]{:S(2)}) copy-start(bf16[256,2048]{1,0:T(8,128)(2,1)} %param.13) | copy-start | bytes 3145732
  67.0 2.0 copy-start.6
  67.0 168.8 %copy-start.7 = (f32[64,512]{1,0:T(8,128)S(1)}, f32[64,512]{1,0:T(8,128)}, u32[]{:S(2)}) copy-start(f32[64,512]{1,0:T(8,128)} %param.19) | copy-start | bytes 393220
  67.0 204.7 %copy-start.4 = (f32[512,64]{0,1:T(8,128)S(1)}, f32[512,64]{0,1:T(8,128)}, u32[]{:S(2)}) copy-start(f32[512,64]{0,1:T(8,128)} %param.16) | copy-start | bytes 393220
  67.0 204.7 %copy-start.8 = (f32[512,64]{0,1:T(8,128)S(1)}, f32[512,64]{0,1:T(8,128)}, u32[]{:S(2)}) copy-start(f32[512,64]{0,1:T(8,128)} %param.18) | copy-start | bytes 393220
  68.9 166.9 %all-reduce.4.cloned.1.call-start = ((), (), s32[]{:S(2)}) async-start(), calls=%async_computation.2 | async-start | bytes 262144 | tf_op jit(solution)/shard_map/psum | solution.py:89
  69.8 201.8 %all-reduce.6.cloned.1.call-start = ((), (), s32[]{:S(2)}) async-start(), calls=%async_computation.4 | async-start | bytes 262144 | tf_op jit(solution)/shard_map/psum | solution.py:81
Sparse Core Ops, SparseCore 0:
  9.9 39.2 all-gather.1
  69.0 35.9 reduce-scatter.1
  111.1 124.5 all-reduce.3
  237.9 33.6 all-reduce.5
where the time goes:
time: 282 us
  waiting for transfers between devices  181 us (64%)
  blocking collectives  50.9 us (18%)
  between operations  16.9 us (6%)
  matrix products  14.2 us (5%)
  other arithmetic  11.1 us (4%)
  local copies, waits for them, and re-layouts  7.48 us (3%)
    psum x1, waiting for transfers between devices, per_device(): lax.psum((adapter_scale * up_term, loss_local, count_local), ('dp', 'fsdp'))  125 us
    psum x1, blocking collectives, per_device(): lax.psum((adapter_scale * up_term, loss_local, count_local), ('dp', 'fsdp'))  39.5 us
    psum x1, waiting for transfers between devices, per_device(): lax.psum(adapter_scale * lax.dot_general(columns, latent_grad, (((0,), (0...  33.7 us
    all_gather x1, waiting for transfers between devices, per_device(): lax.all_gather(value_weight_frozen, 'fsdp', axis=0, tiled=True)  21.2 us
    all_gather x1, blocking collectives, per_device(): lax.all_gather(down_factor_slice, 'fsdp', axis=0, tiled=True)  11.3 us
  transfers between devices with their start and end apart: 4, of which 3 were waited for; matrix products, arithmetic and copies ran while one was open for 4% of the time, Pallas kernels for 0%

commit v1 on v0

--- a/solution.py
+++ b/solution.py
@@ -25,6 +25,11 @@
     average_down_map,
     average_up_map,
 ):
+
+    def supply_positions(u_in):
+        tmp = lax.psum(lax.psum(u_in, axis_name="fsdp"), "dp")
+        return tmp
+
     tok_rows = hidden.shape[0]
     group_size = HEADS // KEY_VALUE_HEADS
     seq_length = lengths[0]
@@ -86,8 +91,8 @@
         "dp",
     )
     down_map_gradient = lax.psum_scatter(down_map_gradient, "fsdp", scatter_dimension=0, tiled=True)
-    up_map_gradient, loss_sum, token_grand_count = lax.psum(
-        (adapter_scale * up_term, loss_local, count_local), ("dp", "fsdp")
+    up_map_gradient, loss_sum, token_grand_count = supply_positions(
+        (adapter_scale * up_term, loss_local, count_local)
     )
     up_map_gradient = up_map_gradient / token_grand_count
     down_map_gradient = down_map_gradient / token_grand_count

time: 282 us -> 211 us (0.75)
  waiting for transfers between devices: 181 us -> 123 us
  blocking collectives: 50.9 us -> 37 us
    psum x1, waiting for transfers between devices: 125 us -> 51.6 us  [supply_positions(): tmp = lax.psum(lax.psum(u_in, axis_name='fsdp'), 'dp')]
    reduce_scatter x1, waiting for transfers between devices: 0.02 us -> 38.6 us  [per_device(): lax.psum_scatter(down_map_gradient, 'fsdp', scatter_dimension=0, tiled=True)]
    psum x1, waiting for transfers between devices: 33.7 us -> 10.9 us  [per_device(): lax.psum(adapter_scale * lax.dot_general(columns, latent_grad, (((0,), (0...]
    psum x1 -> x2, blocking collectives: 39.5 us -> 25.7 us  [supply_positions(): tmp = lax.psum(lax.psum(u_in, axis_name='fsdp'), 'dp')]
  transfers between devices with their start and end apart: 4 -> 4, of which waited for: 3 -> 4; matrix products, arithmetic and copies ran while one was open for 4% -> 5% of each run, Pallas kernels for 0% -> 0%
where the time goes in v1:
time: 211 us; the launch traced here: 210 us
  waiting for transfers between devices  123 us (58%)
  blocking collectives  37 us (18%)
  between operations  17 us (8%)
  matrix products  14.2 us (7%)
  other arithmetic  11.3 us (5%)
  local copies, waits for them, and re-layouts  7.48 us (4%)
    psum x1, waiting for transfers between devices, supply_positions(): tmp = lax.psum(lax.psum(u_in, axis_name='fsdp'), 'dp')  51.6 us
    reduce_scatter x1, waiting for transfers between devices, per_device(): lax.psum_scatter(down_map_gradient, 'fsdp', scatter_dimension=0, tiled=True)  38.6 us
    psum x2, blocking collectives, supply_positions(): tmp = lax.psum(lax.psum(u_in, axis_name='fsdp'), 'dp')  25.7 us
    all_gather x1, waiting for transfers between devices, per_device(): lax.all_gather(value_weight_frozen, 'fsdp', axis=0, tiled=True)  21.2 us
    all_gather x1, blocking collectives, per_device(): lax.all_gather(down_factor_slice, 'fsdp', axis=0, tiled=True)  11.3 us
    psum x1, waiting for transfers between devices, per_device(): lax.psum(adapter_scale * lax.dot_general(columns, latent_grad, (((0,), (0...  10.9 us
  transfers between devices with their start and end apart: 4, of which 4 were waited for; matrix products, arithmetic and copies ran while one was open for 5% of the time, Pallas kernels for 0%

profile of v1, /device:TPU:0, one launch (start us, length us, event | category | flops | bytes accessed | tf_op | source)
XLA Modules:
  0.0 210.2 jit_solution(2461271701099565733)
XLA Ops:
  7.2 0.0 copy-start
  7.2 0.0 copy-start.3
  7.2 0.0 all-gather.2.cloned.1.call-start
  7.2 0.7 all-gather.2.cloned.1.call-update
  7.9 0.0 all-reduce.6.cloned.1.call-start
  8.6 1.8 reshape.40
  10.4 1.0 reshape.39
  11.4 0.0 copy-done.3
  11.5 11.3 %all_gather.7 = bf16[4096,64]{0,1:T(8,128)(2,1)S(1)} all-gather(bf16[512,64]{0,1:T(8,128)(2,1)S(1)} %convert_element_type.36), channel_id=1, replica_groups=mesh['dp'=4,'fsdp'=8] {'fsdp'}, dimensions={0}, use_global_device_ids=true | all-gather | bytes 589824 | tf_op jit(solution)/shard_map/all_gather | solution.py:46
  22.8 0.1 fusion.13
  22.9 0.0 copy-done
  22.9 1.4 convolution_convert_fusion.1
  24.3 0.7 fusion.10
  25.0 1.2 fusion.19
  26.3 1.8 divide_convert_fusion
  28.0 0.0 copy-start.1
  28.0 0.0 copy-start.5
  28.0 21.2 %all-gather.2.cloned.1.call-done = bf16[4096,512]{1,0:T(8,128)(2,1)} async-done(((bf16[512,512]{1,0:T(8,128)(2,1)}), bf16[4096,512]{1,0:T(8,128)(2,1)}) %all-gather.2.cloned.1.call-update) | async-done | bytes 4194320 | tf_op jit(solution)/shard_map/all_gather | solution.py:41
  49.2 3.4 %fusion.20 = f32[256,512]{1,0:T(8,128)S(1)} fusion(bf16[256,4096]{1,0:T(8,128)(2,1)S(1)} %copy-done, bf16[4096,512]{1,0:T(8,128)(2,1)} %all-gather.2.cloned.1.call-done), kind=kOutput, calls=%fused_computation.36 | convolution fusion | flops 1073741824 | bytes 6815744 | tf_op jit(solution)/shard_map/dot_general | solution.py:39
  52.7 0.0 copy-done.1
  52.7 0.0 copy-done.5
  52.7 0.3 fusion.8
  52.9 0.1 copy.27
  53.1 3.3 %fusion.21 = f32[4,128,4,256]{3,1,2,0:T(8,128)} fusion(bf16[256,4,128,1]{0,2,3,1:T(8,128)(2,1)S(1)} %bitcast.51, bf16[4,4,256,256]{2,3,1,0:T(8,128)(2,1)} %divide_convert_fusion), kind=kOutput, calls=%fused_computation.37 | convolution fusion | flops 268435456 | bytes 4456448 | tf_op jit(solution)/shard_map/kgts,skd->tkgd/dot_general | solution.py:67
  56.4 0.0 copy-start.2
  56.4 3.0 %copy.19 = f32[256,2048]{1,0:T(8,128)} copy(f32[256,2048]{0,1:T(8,128)} %bitcast.47) | data formatting | bytes 4194304 | tf_op jit(solution)/shard_map/reshape | solution.py:69
  59.5 0.0 copy-done.2
  59.5 3.6 %multiply_reduce_fusion = (f32[]{:T(128)}, bf16[256,2048]{1,0:T(8,128)(2,1)}) fusion(f32[256,2048]{1,0:T(8,128)} %copy.19, bf16[256,2048]{1,0:T(8,128)(2,1)S(1)} %copy-done.2, pred[256]{0:T(512)(128)(4,1)S(1)} %iota_compare_fusion.1), kind=kLoop, calls=%fused_computation.7 | loop fusion | flops 3145727 | bytes 4194564 | tf_op jit(solution)/shard_map/reduce_sum | solution.py:72
  63.1 1.5 copy.30
  64.6 0.0 copy-start.6
  64.6 2.4 %fusion.9 = bf16[4,128,256]{2,1,0:T(8,128)(2,1)S(1)} fusion(bf16[256,4,4,128]{0,3,2,1:T(8,128)(2,1)S(1)} %bitcast.48, bf16[4,4,256,256]{2,3,1,0:T(8,128)(2,1)} %divide_convert_fusion), kind=kOutput, calls=%fused_computation.17 | convolution fusion | flops 268566528 | bytes 3407872 | tf_op jit(solution)/shard_map/kgts,tkgd->skd/dot_general | solution.py:74
  67.0 0.0 copy-done.6
  67.0 0.9 convolution_multiply_fusion.2
  67.9 0.0 all-reduce.6.cloned.1.call-update
  67.9 0.0 copy-start.7
  67.9 0.0 copy-start.4
  67.9 0.0 copy-start.8
  67.9 0.0 reduce-scatter.2.cloned.1.call-start
  68.0 1.8 fusion.1
  69.8 0.0 reduce-scatter.2.cloned.1.call-update
  69.9 0.0 all-reduce.8.cloned.1.call-start
  69.9 51.6 %all-reduce.6.cloned.1.call-done = f32[64,512]{1,0:T(8,128)} async-done(((f32[64,512]{1,0:T(8,128)}), f32[64,512]{1,0:T(8,128)}) %all-reduce.6.cloned.1.call-update) | async-done | bytes 131088 | tf_op jit(solution)/shard_map/psum | solution.py:30
  121.5 38.6 %reduce-scatter.2.cloned.1.call-done = f32[512,64]{0,1:T(8,128)} async-done(((f32[4096,64]{0,1:T(8,128)}), f32[512,64]{0,1:T(8,128)}) %reduce-scatter.2.cloned.1.call-update) | async-done | bytes 131088 | tf_op jit(solution)/shard_map/reduce_scatter | solution.py:93
  160.0 0.0 all-reduce.8.cloned.1.call-update
  160.1 13.0 %all-reduce = (f32[]{:T(128)}, f32[]{:T(128)}) all-reduce(f32[]{:T(128)S(6)} %convert_element_type.47, f32[]{:T(128)} %get-tuple-element.15), channel_id=1, replica_groups=mesh['dp'=4,'fsdp'=8] {'fsdp'}, use_global_device_ids=true, to_apply=%region_4.5 | all-reduce | flops 2 | bytes 16 | tf_op jit(solution)/shard_map/psum | solution.py:30
  173.0 12.7 %all-reduce.1 = (f32[]{:T(128)}, f32[]{:T(128)}) all-reduce(f32[]{:T(128)} %get-tuple-element.5, f32[]{:T(128)} %get-tuple-element.6), channel_id=1, replica_groups=mesh['dp'=4,'fsdp'=8] {'dp'}, use_global_device_ids=true, to_apply=%region_5.6 | all-reduce | flops 2 | bytes 16 | tf_op jit(solution)/shard_map/psum | solution.py:30
  187.0 10.9 %all-reduce.8.cloned.1.call-done = (f32[512,64]{0,1:T(8,128)}, f32[64,512]{1,0:T(8,128)}) async-done(((f32[512,64]{0,1:T(8,128)}, f32[64,512]{1,0:T(8,128)}), (f32[512,64]{0,1:T(8,128)}, f32[64,512]{1,0:T(8,128)})) %all-reduce.8.cloned.1.call-update) | async-done | bytes 262160 | tf_op jit(solution)/shard_map/psum | solution.py:86
  198.0 0.0 copy-done.7
  198.0 2.3 %multiply_add_fusion = (f32[64,512]{1,0:T(8,128)}, f32[64,512]{1,0:T(8,128)}) fusion(f32[64,512]{1,0:T(8,128)S(1)} %copy-done.1, f32[64,512]{1,0:T(8,128)S(1)} %copy-done.7, f32[64,512]{1,0:T(8,128)} %get-tuple-element.10, f32[]{:T(128)} %get-tuple-element.7), kind=kLoop, calls=%fused_computation.26 | loop fusion | flops 163840 | bytes 655364 | tf_op jit(solution)/shard_map/add | solution.py:103
  200.2 0.0 copy-done.4
  200.2 0.0 copy-done.8
  200.2 2.3 %multiply_add_fusion.1 = (f32[512,64]{0,1:T(8,128)}, f32[512,64]{0,1:T(8,128)}) fusion(f32[512,64]{0,1:T(8,128)S(1)} %copy-done.4, f32[512,64]{0,1:T(8,128)S(1)} %copy-done.8, f32[512,64]{0,1:T(8,128)} %get-tuple-element.9, f32[]{:T(128)} %get-tuple-element.7), kind=kLoop, calls=%fused_computation.27 | loop fusion | flops 163840 | bytes 655364 | tf_op jit(solution)/shard_map/add | solution.py:100
  (2 shorter events, 0.0 us)
Async XLA Ops:
  7.2 15.8 %copy-start = (bf16[256,4096]{1,0:T(8,128)(2,1)S(1)}, bf16[256,4096]{1,0:T(8,128)(2,1)}, u32[]{:S(2)}) copy-start(bf16[256,4096]{1,0:T(8,128)(2,1)} %param.10) | copy-start | bytes 6291460
  7.2 4.3 %copy-start.3 = (f32[512,64]{0,1:T(8,128)S(1)}, f32[512,64]{0,1:T(8,128)}, u32[]{:S(2)}) copy-start(f32[512,64]{0,1:T(8,128)} %param.16) | copy-start | bytes 393220
  7.2 42.0 %all-gather.2.cloned.1.call-start = ((), (), s32[]{:S(2)}) async-start(), calls=%async_computation.1 | async-start | bytes 4718592 | tf_op jit(solution)/shard_map/all_gather | solution.py:41
  7.9 113.5 %all-reduce.6.cloned.1.call-start = ((), (), s32[]{:S(2)}) async-start(), calls=%async_computation.2 | async-start | bytes 262144 | tf_op jit(solution)/shard_map/psum | solution.py:30
  28.0 24.6 %copy-start.1 = (f32[64,512]{1,0:T(8,128)S(1)}, f32[64,512]{1,0:T(8,128)}, u32[]{:S(2)}) copy-start(f32[64,512]{1,0:T(8,128)} %param.17) | copy-start | bytes 393220
  28.0 24.6 %copy-start.5 = (bf16[256,64]{0,1:T(8,128)(2,1)S(1)}, bf16[256,64]{0,1:T(8,128)(2,1)}, u32[]{:S(2)}) copy-start(bf16[256,64]{0,1:T(8,128)(2,1)} %convolution_convert_fusion.1) | copy-start | bytes 98308
  56.4 3.0 %copy-start.2 = (bf16[256,2048]{1,0:T(8,128)(2,1)S(1)}, bf16[256,2048]{1,0:T(8,128)(2,1)}, u32[]{:S(2)}) copy-start(bf16[256,2048]{1,0:T(8,128)(2,1)} %param.13) | copy-start | bytes 3145732
  64.6 2.4 %copy-start.6 = (bf16[256,64]{0,1:T(8,128)(2,1)S(1)}, bf16[256,64]{0,1:T(8,128)(2,1)}, u32[]{:S(2)}) copy-start(bf16[256,64]{0,1:T(8,128)(2,1)} %convolution_convert_fusion.1) | copy-start | bytes 98308
  67.9 130.1 %copy-start.7 = (f32[64,512]{1,0:T(8,128)S(1)}, f32[64,512]{1,0:T(8,128)}, u32[]{:S(2)}) copy-start(f32[64,512]{1,0:T(8,128)} %param.19) | copy-start | bytes 393220
  67.9 132.3 %copy-start.4 = (f32[512,64]{0,1:T(8,128)S(1)}, f32[512,64]{0,1:T(8,128)}, u32[]{:S(2)}) copy-start(f32[512,64]{0,1:T(8,128)} %param.16) | copy-start | bytes 393220
  67.9 132.3 %copy-start.8 = (f32[512,64]{0,1:T(8,128)S(1)}, f32[512,64]{0,1:T(8,128)}, u32[]{:S(2)}) copy-start(f32[512,64]{0,1:T(8,128)} %param.18) | copy-start | bytes 393220
  67.9 92.1 %reduce-scatter.2.cloned.1.call-start = ((), (), s32[]{:S(2)}) async-start(), calls=%async_computation.3 | async-start | bytes 1179648 | tf_op jit(solution)/shard_map/reduce_scatter | solution.py:93
  69.9 128.1 %all-reduce.8.cloned.1.call-start = ((), (), s32[]{:S(2)}) async-start(), calls=%async_computation.4 | async-start | bytes 524288 | tf_op jit(solution)/shard_map/psum | solution.py:86
Sparse Core Ops, SparseCore 0:
  9.9 39.2 all-gather.1
  68.0 53.4 all-reduce.5
  124.7 35.3 reduce-scatter.1
  162.3 35.6 all-reduce.7
